TPU v7x, 128 devices: a whole 4x4x4 slice. The times are simulated.
128 devices in a mesh: tiles: 32 (over x, y, core), reps: 4 (over z).
Axes of the slice: x: 4, y: 4, z: 4, core: 2. Of those that a mesh axis runs over, the one named last changes fastest.
Arguments:
- tiles_w: bfloat16 [4096, 128, 128], P('tiles'), may hold values from 0.0001 to 4
- tile_worker: int32 [4096], P('tiles'), may hold values from 0 to 15
- tile_owner: int32 [4096], P('tiles'), may hold values from 0 to 31
- owner_block: int32 [32, 32], P('tiles'), may hold values from 0 to 1
- worker_base: float32 [65536], P('tiles'), may hold values from -6 to 6
- worker_noise: float32 [65536], P('tiles'), may hold values from 0.2 to 1.5
- worker_cluster: int32 [65536], P('tiles'), may hold values from 0 to 255
- firm_base: float32 [8192], P('tiles'), may hold values from -6 to 6
- firm_noise: float32 [8192], P('tiles'), may hold values from 0.2 to 1.5
- firm_cluster: int32 [8192], P('tiles'), may hold values from 0 to 255
- signs: int32 [256, 256], P('reps'), may hold values from 0 to 1
- covariates: float32 [8192, 512], P('tiles'), may hold values from -0.0625 to 0.0625
- whitening: float32 [512, 512], replicated, may hold values from -0.25 to 0.25
Outputs:
- worker_effect: float32 [256, 65536], P('reps', 'tiles')
- firm_effect: float32 [256, 8192], P('reps', 'tiles')
- coefficients: float32 [256, 512], P('reps')
- covariance: float32 [512, 512], P('tiles')
Inputs may be any that keep to these rules, and one draw needn't show every extreme that they name: `tile_worker`: local worker block of each tile. `tile_owner`: owner of each tile's firm block. `owner_block`: firm block among the owner's 2 blocks. `signs`: a bit that gives the sign 2 b - 1.
All inputs are finite; a program needn't handle non-finite values.
Results may differ from a plain program's by a relative error of at most 0.0023.
Values may be sent and summed in bfloat16 or wider, within the bound.
No kernel may reach another device: no remote copies, remote signals or barrier semaphores. Data moves between devices by JAX's collectives and lax.ppermute only.
A program may use at most 64 MiB of HBM per device.

v0:
```python
import jax
import jax.numpy as jnp
from jax import lax
from jax.sharding import PartitionSpec as P

WORK_BLOCKS = 16
FIRM_BLOCKS = 2
SWEEPS = 6
spectral_bound = 0.8


def chebyshev_weights(sweep_count):
    weights = [1.0]
    weights.append(1.0 / (1.0 - 0.5 * spectral_bound * spectral_bound))
    while len(weights) < sweep_count:
        weights.append(1.0 / (1.0 - 0.25 * spectral_bound * spectral_bound * weights[-1]))
    return weights


def one_hot_rows(indices, row_count):
    return (indices[None, :] == jnp.arange(row_count, dtype=jnp.int32)[:, None]).astype(jnp.float32)


def wild_outcome(base_value, noise_scale, cluster, flip_table):
    clusters_hot = (
        cluster[None, :] == jnp.arange(flip_table.shape[1], dtype=jnp.int32)[:, None]
    ).astype(jnp.bfloat16)
    flip_values = jnp.dot(flip_table, clusters_hot, preferred_element_type=jnp.float32)
    return base_value[None, :] + noise_scale[None, :] * flip_values


def body(
    tiles_w,
    tile_worker,
    tile_owner,
    owner_block,
    worker_base,
    worker_noise,
    worker_cluster,
    firm_base,
    firm_noise,
    firm_cluster,
    signs,
    covariates,
    whitening,
):
    highest = lax.Precision.HIGHEST
    owners_count = lax.axis_size("tiles")
    tile_cells = tiles_w.shape[1]
    replicas_here = signs.shape[0]
    flip_table = (2 * signs - 1).astype(jnp.bfloat16)
    worker_outcome = wild_outcome(worker_base, worker_noise, worker_cluster, flip_table).reshape(
        replicas_here, WORK_BLOCKS, tile_cells
    )
    firm_outcome = wild_outcome(firm_base, firm_noise, firm_cluster, flip_table).reshape(
        replicas_here, FIRM_BLOCKS, tile_cells
    )
    row_mass = jnp.sum(tiles_w, axis=2, dtype=jnp.float32)
    col_mass = jnp.sum(tiles_w, axis=1, dtype=jnp.float32)
    worker_hot = one_hot_rows(tile_worker, WORK_BLOCKS)
    worker_scale = 1.0 + jnp.einsum("bt,tw->bw", worker_hot, row_mass, precision=highest)
    owner_hot = one_hot_rows(tile_owner, owners_count)
    my_blocks = owner_block[0]
    tile_block = tile_owner * FIRM_BLOCKS + jnp.sum(
        jnp.where(owner_hot > 0, my_blocks[:, None], 0), axis=0
    )
    dense_hot = one_hot_rows(tile_block, owners_count * FIRM_BLOCKS)
    firm_mass = lax.psum_scatter(
        jnp.einsum("nt,tf->nf", dense_hot, col_mass, precision=highest),
        "tiles",
        scatter_dimension=0,
        tiled=True,
    )
    firm_scale = 1.0 + firm_mass
    omegas = chebyshev_weights(SWEEPS)
    firm_older = jnp.zeros((replicas_here, FIRM_BLOCKS, tile_cells), jnp.float32)
    firm_newer = firm_older
    firm_now = firm_older
    worker_now = worker_outcome
    tile_firm = None
    for sweep_index in range(SWEEPS):
        if sweep_index == 0:
            worker_now = worker_outcome
        else:
            pulled = jnp.einsum(
                "twf,rtf->rtw", tiles_w, tile_firm, preferred_element_type=jnp.float32
            )
            worker_sum = jnp.einsum("bt,rtw->rbw", worker_hot, pulled, precision=highest)
            worker_now = worker_outcome - worker_sum / worker_scale[None]
        worker_round = worker_now.astype(jnp.bfloat16)
        tile_values = jnp.take(worker_round, tile_worker, axis=1)
        pushed = jnp.einsum(
            "twf,rtw->rtf", tiles_w, tile_values, preferred_element_type=jnp.float32
        )
        firm_sum = lax.psum_scatter(
            jnp.einsum("nt,rtf->rnf", dense_hot, pushed, precision=highest),
            "tiles",
            scatter_dimension=1,
            tiled=True,
        )
        firm_target = firm_outcome - firm_sum / firm_scale[None]
        firm_now = firm_older + omegas[sweep_index] * (firm_target - firm_older)
        firm_older, firm_newer = (firm_newer, firm_now)
        if sweep_index + 1 < SWEEPS:
            firm_round = firm_now.astype(jnp.bfloat16)
            every_firm = lax.all_gather(firm_round, "tiles", axis=1, tiled=True)
            tile_firm = jnp.take(every_firm, tile_block, axis=1)
    worker_effect = worker_now.reshape(replicas_here, WORK_BLOCKS * tile_cells)
    firm_flat = firm_now.reshape(replicas_here, FIRM_BLOCKS * tile_cells)
    mixing = jnp.dot(covariates, whitening.T, precision=highest)
    local_term = jnp.dot(firm_flat, mixing, precision=highest)
    summed = lax.psum(local_term, "tiles")
    share_rows = summed.shape[1] // owners_count
    own_columns = lax.dynamic_slice_in_dim(
        summed, lax.axis_index("tiles") * share_rows, share_rows, 1
    )
    moment = jnp.dot(own_columns.T, summed, precision=highest)
    covariance = lax.psum(moment, "reps") / (replicas_here * lax.axis_size("reps"))
    return (worker_effect, firm_flat, summed, covariance)


def solution(mesh):
    placed = (
        P("tiles", None, None),
        P("tiles"),
        P("tiles"),
        P("tiles", None),
        P("tiles"),
        P("tiles"),
        P("tiles"),
        P("tiles"),
        P("tiles"),
        P("tiles"),
        P("reps", None),
        P("tiles", None),
        P(),
    )
    return jax.shard_map(
        body,
        mesh=mesh,
        in_specs=placed,
        out_specs=(P("reps", "tiles"), P("reps", "tiles"), P("reps", None), P("tiles", None)),
        check_vma=False,
    )
```

profile of v0, /device:TPU:6, one launch (start us, length us, event | category | flops | bytes accessed | tf_op | source)
XLA Modules:
  0.0 1033.3 jit_solution(7390925900868006559)
XLA Ops:
  16.6 4.2 fusion.56
  28.9 109.8 %all-reduce = f32[64,128]{1,0:T(8,128)S(1)} all-reduce(f32[64,128]{1,0:T(8,128)S(1)} %fusion.164), channel_id=3, replica_groups=mesh['tiles'=32,'reps'=4] {'tiles'}, use_global_device_ids=true, to_apply=%region_3.0.clone | all-reduce | flops 8192 | bytes 65536
  140.8 57.8 %all-gather.6.cloned.1.call-done = bf16[64,64,128]{2,0,1:T(8,128)(2,1)} async-done(((bf16[64,2,128]{2,0,1:T(8,128)(2,1)}), bf16[64,64,128]{2,0,1:T(8,128)(2,1)}) %all-gather.6.cloned.1.call-update) | async-done | bytes 1048592 | tf_op jit(solution)/shard_map/all_gather | solution.py:106
  202.0 5.8 convolution_bitcast_fusion.9
  217.9 4.2 fusion.59
  225.1 78.4 %reduce-scatter.9.cloned.1.call-done = f32[64,2,128]{2,0,1:T(8,128)} async-done(((f32[64,64,128]{2,0,1:T(8,128)}), f32[64,2,128]{2,0,1:T(8,128)}) %reduce-scatter.9.cloned.1.call-update) | async-done | bytes 65552 | tf_op jit(solution)/shard_map/reduce_scatter | solution.py:95
  305.0 43.0 %all-gather.8.cloned.1.call-done = bf16[64,64,128]{2,0,1:T(8,128)(2,1)} async-done(((bf16[64,2,128]{2,0,1:T(8,128)(2,1)}), bf16[64,64,128]{2,0,1:T(8,128)(2,1)}) %all-gather.8.cloned.1.call-update) | async-done | bytes 1048592 | tf_op jit(solution)/shard_map/all_gather | solution.py:106
  351.3 5.8 convolution_bitcast_fusion.7
  367.3 4.2 fusion.62
  374.2 78.4 %reduce-scatter.11.cloned.1.call-done = f32[64,2,128]{2,0,1:T(8,128)} async-done(((f32[64,64,128]{2,0,1:T(8,128)}), f32[64,2,128]{2,0,1:T(8,128)}) %reduce-scatter.11.cloned.1.call-update) | async-done | bytes 65552 | tf_op jit(solution)/shard_map/reduce_scatter | solution.py:95
  454.2 43.0 %all-gather.10.cloned.1.call-done = bf16[64,64,128]{2,0,1:T(8,128)(2,1)} async-done(((bf16[64,2,128]{2,0,1:T(8,128)(2,1)}), bf16[64,64,128]{2,0,1:T(8,128)(2,1)}) %all-gather.10.cloned.1.call-update) | async-done | bytes 1048592 | tf_op jit(solution)/shard_map/all_gather | solution.py:106
  500.5 5.7 convolution_bitcast_fusion.5
  516.4 4.2 fusion.65
  523.6 78.4 %reduce-scatter.13.cloned.1.call-done = f32[64,2,128]{2,0,1:T(8,128)} async-done(((f32[64,64,128]{2,0,1:T(8,128)}), f32[64,2,128]{2,0,1:T(8,128)}) %reduce-scatter.13.cloned.1.call-update) | async-done | bytes 65552 | tf_op jit(solution)/shard_map/reduce_scatter | solution.py:95
  603.5 43.1 %all-gather.12.cloned.1.call-done = bf16[64,64,128]{2,0,1:T(8,128)(2,1)} async-done(((bf16[64,2,128]{2,0,1:T(8,128)(2,1)}), bf16[64,64,128]{2,0,1:T(8,128)(2,1)}) %all-gather.12.cloned.1.call-update) | async-done | bytes 1048592 | tf_op jit(solution)/shard_map/all_gather | solution.py:106
  650.0 5.8 convolution_bitcast_fusion.3
  665.9 4.2 fusion.68
  672.9 78.4 %reduce-scatter.15.cloned.1.call-done = f32[64,2,128]{2,0,1:T(8,128)} async-done(((f32[64,64,128]{2,0,1:T(8,128)}), f32[64,2,128]{2,0,1:T(8,128)}) %reduce-scatter.15.cloned.1.call-update) | async-done | bytes 65552 | tf_op jit(solution)/shard_map/reduce_scatter | solution.py:95
  752.8 43.0 %all-gather.14.cloned.1.call-done = bf16[64,64,128]{2,0,1:T(8,128)(2,1)} async-done(((bf16[64,2,128]{2,0,1:T(8,128)(2,1)}), bf16[64,64,128]{2,0,1:T(8,128)(2,1)}) %all-gather.14.cloned.1.call-update) | async-done | bytes 1048592 | tf_op jit(solution)/shard_map/all_gather | solution.py:106
  799.1 5.8 convolution_bitcast_fusion.1
  815.1 4.2 fusion.71
  824.1 76.3 %reduce-scatter.17.cloned.1.call-done = f32[64,2,128]{2,0,1:T(8,128)} async-done(((f32[64,64,128]{2,0,1:T(8,128)}), f32[64,2,128]{2,0,1:T(8,128)}) %reduce-scatter.17.cloned.1.call-update) | async-done | bytes 65552 | tf_op jit(solution)/shard_map/reduce_scatter | solution.py:95
  903.4 102.1 %all-reduce.3.cloned.1.call-done = f32[64,512]{1,0:T(8,128)} async-done(((f32[64,512]{1,0:T(8,128)}), f32[64,512]{1,0:T(8,128)}) %all-reduce.3.cloned.1.call-update) | async-done | bytes 131088 | tf_op jit(solution)/shard_map/psum | solution.py:112
  1006.8 17.3 %psum.15 = f32[16,512]{1,0:T(8,128)S(1)} all-reduce(f32[16,512]{1,0:T(8,128)S(1)} %fusion.162), channel_id=1, replica_groups=mesh['tiles'=32,'reps'=4] {'reps'}, use_global_device_ids=true, to_apply=%region_11.14 | all-reduce | flops 8192 | bytes 65536 | tf_op jit(solution)/shard_map/psum | solution.py:118
  (113 shorter events, 115.5 us)
Async XLA Ops:
  7.2 814.9 %copy-start = (f32[512,512]{1,0:T(8,128)S(1)}, f32[512,512]{1,0:T(8,128)}, u32[]{:S(2)}) copy-start(f32[512,512]{1,0:T(8,128)} %param.29) | copy-start | bytes 3145732
  7.2 3.1 copy-start.11
  7.2 3.1 copy-start.6
  7.2 131.7 %reduce-scatter.7.cloned.1.call-start = ((), (), s32[]{:S(2)}) async-start(), calls=%async_computation.6 | async-start | bytes 2162688 | tf_op jit(solution)/shard_map/reduce_scatter | solution.py:95
  23.4 175.2 %all-gather.6.cloned.1.call-start = ((), (), s32[]{:S(2)}) async-start(), calls=%async_computation.7 | async-start | bytes 1081344 | tf_op jit(solution)/shard_map/all_gather | solution.py:106
  25.2 113.4 %copy-start.7 = (s32[64,256]{1,0:T(8,128)S(1)}, s32[64,256]{1,0:T(8,128)}, u32[]{:S(2)}) copy-start(s32[64,256]{1,0:T(8,128)} %param.27) | copy-start | bytes 196612
  25.2 113.4 %copy-start.8 = (s32[256]{0:T(256)S(1)}, s32[256]{0:T(256)}, u32[]{:S(2)}) copy-start(s32[256]{0:T(256)} %param.26) | copy-start | bytes 3076
  25.2 113.4 %copy-start.9 = (f32[256]{0:T(256)S(1)}, f32[256]{0:T(256)}, u32[]{:S(2)}) copy-start(f32[256]{0:T(256)} %param.25) | copy-start | bytes 3076
  25.3 113.4 %copy-start.10 = (f32[256]{0:T(256)S(1)}, f32[256]{0:T(256)}, u32[]{:S(2)}) copy-start(f32[256]{0:T(256)} %param.24) | copy-start | bytes 3076
  25.3 115.4 %copy-start.5 = (s32[128]{0:T(128)S(1)}, s32[128]{0:T(128)}, u32[]{:S(2)}) copy-start(s32[128]{0:T(128)} %param.18) | copy-start | bytes 1540
  140.4 163.1 %reduce-scatter.9.cloned.1.call-start = ((), (), s32[]{:S(2)}) async-start(), calls=%async_computation.8 | async-start | bytes 2162688 | tf_op jit(solution)/shard_map/reduce_scatter | solution.py:95
  225.0 122.9 %all-gather.8.cloned.1.call-start = ((), (), s32[]{:S(2)}) async-start(), calls=%async_computation.9 | async-start | bytes 1081344 | tf_op jit(solution)/shard_map/all_gather | solution.py:106
  305.0 147.6 %reduce-scatter.11.cloned.1.call-start = ((), (), s32[]{:S(2)}) async-start(), calls=%async_computation.10 | async-start | bytes 2162688 | tf_op jit(solution)/shard_map/reduce_scatter | solution.py:95
  374.2 78.4 %copy-start.2 = (f32[64,2,128]{2,0,1:T(8,128)S(1)}, f32[64,2,128]{2,0,1:T(8,128)}, u32[]{:S(2)}) copy-start(f32[64,2,128]{2,0,1:T(8,128)} %reduce-scatter.7.cloned.1.call-done) | copy-start | bytes 196612
  374.2 122.9 %all-gather.10.cloned.1.call-start = ((), (), s32[]{:S(2)}) async-start(), calls=%async_computation.11 | async-start | bytes 1081344 | tf_op jit(solution)/shard_map/all_gather | solution.py:106
  454.1 147.9 %reduce-scatter.13.cloned.1.call-start = ((), (), s32[]{:S(2)}) async-start(), calls=%async_computation.12 | async-start | bytes 2162688 | tf_op jit(solution)/shard_map/reduce_scatter | solution.py:95
  523.5 78.4 %copy-start.3 = (f32[64,2,128]{2,0,1:T(8,128)S(1)}, f32[64,2,128]{2,0,1:T(8,128)}, u32[]{:S(2)}) copy-start(f32[64,2,128]{2,0,1:T(8,128)} %reduce-scatter.9.cloned.1.call-done) | copy-start | bytes 196612
  523.6 123.1 %all-gather.12.cloned.1.call-start = ((), (), s32[]{:S(2)}) async-start(), calls=%async_computation.13 | async-start | bytes 1081344 | tf_op jit(solution)/shard_map/all_gather | solution.py:106
  603.5 147.8 %reduce-scatter.15.cloned.1.call-start = ((), (), s32[]{:S(2)}) async-start(), calls=%async_computation.14 | async-start | bytes 2162688 | tf_op jit(solution)/shard_map/reduce_scatter | solution.py:95
  672.9 122.9 %all-gather.14.cloned.1.call-start = ((), (), s32[]{:S(2)}) async-start(), calls=%async_computation.15 | async-start | bytes 1081344 | tf_op jit(solution)/shard_map/all_gather | solution.py:106
  752.8 147.7 %reduce-scatter.17.cloned.1.call-start = ((), (), s32[]{:S(2)}) async-start(), calls=%async_computation.16 | async-start | bytes 2162688 | tf_op jit(solution)/shard_map/reduce_scatter | solution.py:95
  822.0 1.0 copy-start.1
  822.0 183.5 %all-reduce.3.cloned.1.call-start = ((), (), s32[]{:S(2)}) async-start(), calls=%async_computation.17 | async-start | bytes 262144 | tf_op jit(solution)/shard_map/psum | solution.py:112
  901.3 124.9 %copy-start.4 = (f32[64,256]{1,0:T(8,128)}, f32[64,256]{1,0:T(8,128)S(1)}, u32[]{:S(2)}) copy-start(f32[64,256]{1,0:T(8,128)S(1)} %copy_bitcast_fusion.1) | copy-start | bytes 196612
  (1 other events, 0.7 us)
Sparse Core Ops, SparseCore 0:
  23.5 80.7 reduce-scatter.6
  140.5 58.0 all-gather.5
  225.2 78.2 reduce-scatter.8
  306.1 41.7 all-gather.7
  374.3 78.2 reduce-scatter.10
  455.3 41.7 all-gather.9
  523.7 78.2 reduce-scatter.12
  604.8 41.7 all-gather.11
  673.0 78.2 reduce-scatter.14
  753.9 41.7 all-gather.13
  822.2 78.2 reduce-scatter.16
  904.1 101.3 all-reduce.2
where the time goes:
time: 1040 us; the launch traced here: 1030 us
  waiting for transfers between devices  722 us (69%)
  blocking collectives  127 us (12%)
  matrix products  103 us (10%)
  local copies, waits for them, and re-layouts  51.7 us (5%)
  between operations  15.5 us (1%)
  other arithmetic  13.9 us (1%)
    reduce_scatter x6, waiting for transfers between devices, body(): lax.psum_scatter(jnp.einsum('nt,rtf->rnf', dense_hot, pushed, precision=h...  390 us
    all_gather x5, waiting for transfers between devices, body(): every_firm = lax.all_gather(firm_round, 'tiles', axis=1, tiled=True)  230 us
    unnamed x1, blocking collectives  110 us
    psum x1, waiting for transfers between devices, body(): summed = lax.psum(local_term, 'tiles')  102 us
    dot_general x5, matrix products, body(): jnp.einsum('twf,rtf->rtw', tiles_w, tile_firm, preferred_element_type=jnp...  28.7 us
    dot_general x6, matrix products, body(): jnp.einsum('nt,rtf->rnf', dense_hot, pushed, precision=highest)  24.9 us
    dot_general x6, matrix products, body(): jnp.einsum('twf,rtw->rtf', tiles_w, tile_values, preferred_element_type=j...  24.6 us
  transfers between devices with their start and end apart: 12, of which 11 were waited for; matrix products, arithmetic and copies ran while one was open for 1% of the time, Pallas kernels for 0%

commit v1 on v0

--- a/solution.py
+++ b/solution.py
@@ -2,6 +2,7 @@
 import jax.numpy as jnp
 from jax import lax
 from jax.sharding import PartitionSpec as P
+from jax.lax import all_gather
 
 WORK_BLOCKS = 16
 FIRM_BLOCKS = 2
@@ -103,7 +104,8 @@
         firm_older, firm_newer = (firm_newer, firm_now)
         if sweep_index + 1 < SWEEPS:
             firm_round = firm_now.astype(jnp.bfloat16)
-            every_firm = lax.all_gather(firm_round, "tiles", axis=1, tiled=True)
+            work_now = all_gather(firm_round, "tiles")
+            every_firm = jnp.concatenate(work_now, axis=1)
             tile_firm = jnp.take(every_firm, tile_block, axis=1)
     worker_effect = worker_now.reshape(replicas_here, WORK_BLOCKS * tile_cells)
     firm_flat = firm_now.reshape(replicas_here, FIRM_BLOCKS * tile_cells)

time: 1040 us -> 1040 us (level)
  no operation moved by 1% of the time
where the time goes in v1:
time: 1040 us; the launch traced here: 1030 us
  waiting for transfers between devices  722 us (69%)
  blocking collectives  127 us (12%)
  matrix products  103 us (10%)
  local copies, waits for them, and re-layouts  56.1 us (5%)
  between operations  15.6 us (2%)
  other arithmetic  10.8 us (1%)
    reduce_scatter x6, waiting for transfers between devices, body(): lax.psum_scatter(jnp.einsum('nt,rtf->rnf', dense_hot, pushed, precision=h...  390 us
    all_gather x5, waiting for transfers between devices, body(): work_now = all_gather(firm_round, 'tiles')  230 us
    unnamed x1, blocking collectives  110 us
    psum x1, waiting for transfers between devices, body(): summed = lax.psum(local_term, 'tiles')  102 us
    dot_general x5, matrix products, body(): jnp.einsum('twf,rtf->rtw', tiles_w, tile_firm, preferred_element_type=jnp...  28.8 us
    dot_general x6, matrix products, body(): jnp.einsum('nt,rtf->rnf', dense_hot, pushed, precision=highest)  24.9 us
    dot_general x6, matrix products, body(): jnp.einsum('twf,rtw->rtf', tiles_w, tile_values, preferred_element_type=j...  24.6 us
  transfers between devices with their start and end apart: 12, of which 11 were waited for; matrix products, arithmetic and copies ran while one was open for 1% of the time, Pallas kernels for 0%

profile of v1, /device:TPU:6, one launch (start us, length us, event | category | flops | bytes accessed | tf_op | source)
XLA Modules:
  0.0 1034.6 jit_solution(8647276553938843925)
XLA Ops:
  16.6 4.2 fusion.56
  28.9 109.8 %all-reduce = f32[64,128]{1,0:T(8,128)S(1)} all-reduce(f32[64,128]{1,0:T(8,128)S(1)} %fusion.164), channel_id=8, replica_groups=mesh['tiles'=32,'reps'=4] {'tiles'}, use_global_device_ids=true, to_apply=%region_3.0.clone | all-reduce | flops 8192 | bytes 65536
  140.8 57.8 %all-gather.11.cloned.1.call-done = bf16[2048,2,128]{2,1,0:T(2,128)(2,1)} async-done(((bf16[64,2,128]{2,1,0:T(2,128)(2,1)}), bf16[2048,2,128]{2,1,0:T(2,128)(2,1)}) %all-gather.11.cloned.1.call-update) | async-done | bytes 1048592 | tf_op jit(solution)/shard_map/all_gather | solution.py:107
  202.3 5.8 convolution_bitcast_fusion.9
  218.2 4.2 fusion.59
  225.4 78.3 %reduce-scatter.9.cloned.1.call-done = f32[64,2,128]{2,0,1:T(8,128)} async-done(((f32[64,64,128]{2,0,1:T(8,128)}), f32[64,2,128]{2,0,1:T(8,128)}) %reduce-scatter.9.cloned.1.call-update) | async-done | bytes 65552 | tf_op jit(solution)/shard_map/reduce_scatter | solution.py:96
  305.3 43.0 %all-gather.13.cloned.1.call-done = bf16[2048,2,128]{2,1,0:T(2,128)(2,1)} async-done(((bf16[64,2,128]{2,1,0:T(2,128)(2,1)}), bf16[2048,2,128]{2,1,0:T(2,128)(2,1)}) %all-gather.13.cloned.1.call-update) | async-done | bytes 1048592 | tf_op jit(solution)/shard_map/all_gather | solution.py:107
  351.9 5.8 convolution_bitcast_fusion.7
  367.8 4.2 fusion.62
  374.8 78.3 %reduce-scatter.11.cloned.1.call-done = f32[64,2,128]{2,0,1:T(8,128)} async-done(((f32[64,64,128]{2,0,1:T(8,128)}), f32[64,2,128]{2,0,1:T(8,128)}) %reduce-scatter.11.cloned.1.call-update) | async-done | bytes 65552 | tf_op jit(solution)/shard_map/reduce_scatter | solution.py:96
  454.7 42.9 %all-gather.15.cloned.1.call-done = bf16[2048,2,128]{2,1,0:T(2,128)(2,1)} async-done(((bf16[64,2,128]{2,1,0:T(2,128)(2,1)}), bf16[2048,2,128]{2,1,0:T(2,128)(2,1)}) %all-gather.15.cloned.1.call-update) | async-done | bytes 1048592 | tf_op jit(solution)/shard_map/all_gather | solution.py:107
  501.3 5.8 convolution_bitcast_fusion.5
  517.2 4.2 fusion.65
  524.4 78.4 %reduce-scatter.13.cloned.1.call-done = f32[64,2,128]{2,0,1:T(8,128)} async-done(((f32[64,64,128]{2,0,1:T(8,128)}), f32[64,2,128]{2,0,1:T(8,128)}) %reduce-scatter.13.cloned.1.call-update) | async-done | bytes 65552 | tf_op jit(solution)/shard_map/reduce_scatter | solution.py:96
  604.3 43.1 %all-gather.17.cloned.1.call-done = bf16[2048,2,128]{2,1,0:T(2,128)(2,1)} async-done(((bf16[64,2,128]{2,1,0:T(2,128)(2,1)}), bf16[2048,2,128]{2,1,0:T(2,128)(2,1)}) %all-gather.17.cloned.1.call-update) | async-done | bytes 1048592 | tf_op jit(solution)/shard_map/all_gather | solution.py:107
  651.0 5.8 convolution_bitcast_fusion.3
  667.0 4.2 fusion.68
  673.9 78.4 %reduce-scatter.15.cloned.1.call-done = f32[64,2,128]{2,0,1:T(8,128)} async-done(((f32[64,64,128]{2,0,1:T(8,128)}), f32[64,2,128]{2,0,1:T(8,128)}) %reduce-scatter.15.cloned.1.call-update) | async-done | bytes 65552 | tf_op jit(solution)/shard_map/reduce_scatter | solution.py:96
  753.9 42.9 %all-gather.19.cloned.1.call-done = bf16[2048,2,128]{2,1,0:T(2,128)(2,1)} async-done(((bf16[64,2,128]{2,1,0:T(2,128)(2,1)}), bf16[2048,2,128]{2,1,0:T(2,128)(2,1)}) %all-gather.19.cloned.1.call-update) | async-done | bytes 1048592 | tf_op jit(solution)/shard_map/all_gather | solution.py:107
  800.4 5.8 convolution_bitcast_fusion.1
  816.3 4.2 fusion.71
  825.4 76.3 %reduce-scatter.17.cloned.1.call-done = f32[64,2,128]{2,0,1:T(8,128)} async-done(((f32[64,64,128]{2,0,1:T(8,128)}), f32[64,2,128]{2,0,1:T(8,128)}) %reduce-scatter.17.cloned.1.call-update) | async-done | bytes 65552 | tf_op jit(solution)/shard_map/reduce_scatter | solution.py:96
  904.6 102.2 %all-reduce.3.cloned.1.call-done = f32[64,512]{1,0:T(8,128)} async-done(((f32[64,512]{1,0:T(8,128)}), f32[64,512]{1,0:T(8,128)}) %all-reduce.3.cloned.1.call-update) | async-done | bytes 131088 | tf_op jit(solution)/shard_map/psum | solution.py:114
  1008.1 17.3 %psum.15 = f32[16,512]{1,0:T(8,128)S(1)} all-reduce(f32[16,512]{1,0:T(8,128)S(1)} %fusion.162), channel_id=1, replica_groups=mesh['tiles'=32,'reps'=4] {'reps'}, use_global_device_ids=true, to_apply=%region_11.14 | all-reduce | flops 8192 | bytes 65536 | tf_op jit(solution)/shard_map/psum | solution.py:120
  (128 shorter events, 116.8 us)
Async XLA Ops:
  7.2 816.2 %copy-start = (f32[512,512]{1,0:T(8,128)S(1)}, f32[512,512]{1,0:T(8,128)}, u32[]{:S(2)}) copy-start(f32[512,512]{1,0:T(8,128)} %param.29) | copy-start | bytes 3145732
  7.2 3.1 copy-start.11
  7.2 3.1 copy-start.6
  7.2 131.7 %reduce-scatter.7.cloned.1.call-start = ((), (), s32[]{:S(2)}) async-start(), calls=%async_computation.6 | async-start | bytes 2162688 | tf_op jit(solution)/shard_map/reduce_scatter | solution.py:96
  23.4 175.3 %all-gather.11.cloned.1.call-start = ((), (), s32[]{:S(2)}) async-start(), calls=%async_computation.13 | async-start | bytes 1081344 | tf_op jit(solution)/shard_map/all_gather | solution.py:107
  25.2 113.5 %copy-start.7 = (s32[64,256]{1,0:T(8,128)S(1)}, s32[64,256]{1,0:T(8,128)}, u32[]{:S(2)}) copy-start(s32[64,256]{1,0:T(8,128)} %param.27) | copy-start | bytes 196612
  25.2 113.5 %copy-start.8 = (s32[256]{0:T(256)S(1)}, s32[256]{0:T(256)}, u32[]{:S(2)}) copy-start(s32[256]{0:T(256)} %param.26) | copy-start | bytes 3076
  25.2 113.5 %copy-start.9 = (f32[256]{0:T(256)S(1)}, f32[256]{0:T(256)}, u32[]{:S(2)}) copy-start(f32[256]{0:T(256)} %param.25) | copy-start | bytes 3076
  25.3 113.5 %copy-start.10 = (f32[256]{0:T(256)S(1)}, f32[256]{0:T(256)}, u32[]{:S(2)}) copy-start(f32[256]{0:T(256)} %param.24) | copy-start | bytes 3076
  25.3 115.4 %copy-start.5 = (s32[128]{0:T(128)S(1)}, s32[128]{0:T(128)}, u32[]{:S(2)}) copy-start(s32[128]{0:T(128)} %param.18) | copy-start | bytes 1540
  140.4 163.3 %reduce-scatter.9.cloned.1.call-start = ((), (), s32[]{:S(2)}) async-start(), calls=%async_computation.7 | async-start | bytes 2162688 | tf_op jit(solution)/shard_map/reduce_scatter | solution.py:96
  225.3 122.9 %all-gather.13.cloned.1.call-start = ((), (), s32[]{:S(2)}) async-start(), calls=%async_computation.14 | async-start | bytes 1081344 | tf_op jit(solution)/shard_map/all_gather | solution.py:107
  305.2 147.8 %reduce-scatter.11.cloned.1.call-start = ((), (), s32[]{:S(2)}) async-start(), calls=%async_computation.8 | async-start | bytes 2162688 | tf_op jit(solution)/shard_map/reduce_scatter | solution.py:96
  374.7 78.4 %copy-start.2 = (f32[64,2,128]{2,0,1:T(8,128)S(1)}, f32[64,2,128]{2,0,1:T(8,128)}, u32[]{:S(2)}) copy-start(f32[64,2,128]{2,0,1:T(8,128)} %reduce-scatter.7.cloned.1.call-done) | copy-start | bytes 196612
  374.7 122.9 %all-gather.15.cloned.1.call-start = ((), (), s32[]{:S(2)}) async-start(), calls=%async_computation.15 | async-start | bytes 1081344 | tf_op jit(solution)/shard_map/all_gather | solution.py:107
  454.6 148.1 %reduce-scatter.13.cloned.1.call-start = ((), (), s32[]{:S(2)}) async-start(), calls=%async_computation.9 | async-start | bytes 2162688 | tf_op jit(solution)/shard_map/reduce_scatter | solution.py:96
  524.3 78.4 %copy-start.3 = (f32[64,2,128]{2,0,1:T(8,128)S(1)}, f32[64,2,128]{2,0,1:T(8,128)}, u32[]{:S(2)}) copy-start(f32[64,2,128]{2,0,1:T(8,128)} %reduce-scatter.9.cloned.1.call-done) | copy-start | bytes 196612
  524.3 123.1 %all-gather.17.cloned.1.call-start = ((), (), s32[]{:S(2)}) async-start(), calls=%async_computation.16 | async-start | bytes 1081344 | tf_op jit(solution)/shard_map/all_gather | solution.py:107
  604.3 148.0 %reduce-scatter.15.cloned.1.call-start = ((), (), s32[]{:S(2)}) async-start(), calls=%async_computation.10 | async-start | bytes 2162688 | tf_op jit(solution)/shard_map/reduce_scatter | solution.py:96
  673.9 122.9 %all-gather.19.cloned.1.call-start = ((), (), s32[]{:S(2)}) async-start(), calls=%async_computation.17 | async-start | bytes 1081344 | tf_op jit(solution)/shard_map/all_gather | solution.py:107
  753.8 147.9 %reduce-scatter.17.cloned.1.call-start = ((), (), s32[]{:S(2)}) async-start(), calls=%async_computation.11 | async-start | bytes 2162688 | tf_op jit(solution)/shard_map/reduce_scatter | solution.py:96
  823.3 1.0 copy-start.1
  823.3 183.5 %all-reduce.3.cloned.1.call-start = ((), (), s32[]{:S(2)}) async-start(), calls=%async_computation.12 | async-start | bytes 262144 | tf_op jit(solution)/shard_map/psum | solution.py:114
  902.6 125.0 %copy-start.4 = (f32[64,256]{1,0:T(8,128)}, f32[64,256]{1,0:T(8,128)S(1)}, u32[]{:S(2)}) copy-start(f32[64,256]{1,0:T(8,128)S(1)} %copy_bitcast_fusion.1) | copy-start | bytes 196612
  (1 other events, 0.7 us)
Sparse Core Ops, SparseCore 0:
  23.5 80.8 reduce-scatter.6
  140.6 58.0 all-gather.10
  225.5 78.2 reduce-scatter.8
  306.4 41.8 all-gather.12
  374.8 78.2 reduce-scatter.10
  455.8 41.8 all-gather.14
  524.5 78.2 reduce-scatter.12
  605.6 41.7 all-gather.16
  674.0 78.2 reduce-scatter.14
  755.0 41.7 all-gather.18
  823.4 78.2 reduce-scatter.16
  905.3 101.4 all-reduce.2
